TPU v7x, 128 devices: a whole 4x4x4 slice. The times are simulated.
128 devices in a mesh: ep: 8 (over z_lo, x), fsdp: 16 (over z_hi, y, core).
Axes of the slice: x: 4, y: 4, z: 4 (z_hi: 2, z_lo: 2; z = z_hi * 2 + z_lo), core: 2. Of those that a mesh axis runs over, the one named last changes fastest.
Arguments:
- train_gate: float32 [64, 2048, 1408], P('ep', 'fsdp'), may hold values from -0.1875 to 0.1875
- other_gate: bfloat16 [64, 2048, 1408], P('ep', 'fsdp'), may hold values from -0.0625 to 0.0625
- train_up: float32 [64, 2048, 1408], P('ep', 'fsdp'), may hold values from -0.1875 to 0.1875
- other_up: bfloat16 [64, 2048, 1408], P('ep', 'fsdp'), may hold values from -0.0625 to 0.0625
- router_weight: float32 [2048, 64], P('fsdp', 'ep'), may hold values from -0.125 to 0.125
- router_gain: float32 [2048], P('fsdp'), may hold values from 0.25 to 1.75
Outputs:
- ready_gate: bfloat16 [64, 2048, 1408], P('ep', None, 'fsdp')
- ready_up: bfloat16 [64, 2048, 1408], P('ep', None, 'fsdp')
- scale_gate: float32 [64, 1408], P('ep', 'fsdp')
- scale_up: float32 [64, 1408], P('ep', 'fsdp')
- serve_router: bfloat16 [2048, 64], replicated
All inputs are finite; a program needn't handle non-finite values. Where the computation divides by a largest or mean magnitude, that divisor is 1e-20 or more.
Results may differ from a plain program's by a relative error of at most 0.001.
Values may be sent and summed in bfloat16 or wider, within the bound.
A program may use at most 128 MiB of HBM per device.

v0:
```python
import jax
import jax.numpy as jnp
from jax import lax
from jax.sharding import Mesh
from jax.sharding import PartitionSpec as P

EP = ("ep_0", "ep_1")


def sent_to_all(array, axis):
    peers = lax.axis_size(axis)
    return lax.all_to_all(
        jnp.broadcast_to(array[None], (peers, *array.shape)), axis, 0, 0, tiled=True
    )


def taken_together(array, axis):
    everything = sent_to_all(array, axis)
    return jnp.max(everything, axis=0)


def in_one(arrays, axis):
    flat, at, finished = (jnp.concatenate([a.reshape(-1) for a in arrays]), 0, [])
    total = taken_together(flat, axis)
    for a in arrays:
        finished.append(total[at : at + a.size].reshape(a.shape))
        at += a.size
    return tuple(finished)


def side_by_side(arrays, axis, split_dim, concat_dim, along):
    widths = [a.shape[along] for a in arrays]
    both = jnp.concatenate(arrays, axis=along)
    filled = lax.all_to_all(both, axis, split_axis=split_dim, concat_axis=concat_dim, tiled=True)
    return tuple(jnp.split(filled, [sum(widths[:k]) for k in range(1, len(widths))], axis=along))


def joined_along(parts, dim):
    lengths = list(parts.shape[1:])
    lengths[dim] *= parts.shape[0]
    return jnp.moveaxis(parts, 0, dim).reshape(lengths)


def gathered_copies(array, axis, dim):
    parts = sent_to_all(array, axis)
    return joined_along(parts, dim)


def stacked_from(array, axes, order):
    parts = array[None]
    for k in order:
        parts = lax.all_gather(parts, axes[k], axis=0, tiled=True)
    carried = [lax.axis_size(axes[k]) for k in reversed(order)]
    parts = parts.reshape(*carried, *array.shape)
    turned = sorted(range(len(order)), key=lambda place: order[len(order) - 1 - place])
    return parts.transpose(*turned, *range(len(order), parts.ndim)).reshape(-1, *array.shape)


def gather_axes(array, axes, order, dim):
    return joined_along(stacked_from(array, axes, order), dim)


def per_device(train_gate, other_gate, train_up, other_up, router_weight, router_gain):
    latest_gate = train_gate + other_gate.astype(jnp.float32)
    latest_up = train_up + other_up.astype(jnp.float32)
    scale_gate, scale_up = in_one(
        (jnp.max(jnp.abs(latest_gate), axis=1), jnp.max(jnp.abs(latest_up), axis=1)), "fsdp"
    )
    narrow_gate, narrow_up = (
        (latest_gate / jnp.expand_dims(scale_gate, 1)).astype(jnp.bfloat16),
        (latest_up / jnp.expand_dims(scale_up, 1)).astype(jnp.bfloat16),
    )
    ready_gate, ready_up = side_by_side((narrow_gate, narrow_up), "fsdp", 2, 1, 0)
    scale_gate = lax.dynamic_slice_in_dim(
        scale_gate, lax.axis_index("fsdp") * ready_gate.shape[2], ready_gate.shape[2], axis=1
    )
    scale_up = lax.dynamic_slice_in_dim(
        scale_up, lax.axis_index("fsdp") * ready_up.shape[2], ready_up.shape[2], axis=1
    )
    part_router = (router_weight * router_gain[:, None]).astype(jnp.bfloat16)
    row_router = gathered_copies(part_router, "fsdp", 0)
    serve_router = gather_axes(row_router, EP, (0, 1), 1)
    return (ready_gate, ready_up, scale_gate, scale_up, serve_router)


def solution(mesh):
    split = Mesh(mesh.devices.reshape(2, 4, mesh.shape["fsdp"]), ("ep_0", "ep_1", "fsdp"))
    return jax.shard_map(
        per_device,
        mesh=split,
        in_specs=(
            P(EP, "fsdp", None),
            P(EP, "fsdp", None),
            P(EP, "fsdp", None),
            P(EP, "fsdp", None),
            P("fsdp", EP),
            P("fsdp"),
        ),
        out_specs=(P(EP, None, "fsdp"), P(EP, None, "fsdp"), P(EP, "fsdp"), P(EP, "fsdp"), P()),
        check_vma=False,
    )
```

profile of v0, /device:TPU:8, one launch (start us, length us, event | category | flops | bytes accessed | tf_op | source)
XLA Modules:
  0.0 182.9 jit_solution(4989648456742953288)
XLA Ops:
  0.6 6.5 %copy.69 = f32[8,128,1408]{1,0,2:T(8,128)} copy(f32[8,128,1408]{2,1,0:T(8,128)} %param.6) | data formatting | bytes 11534336 | tf_op args[0]
  7.1 4.1 %copy.68 = bf16[8,128,1408]{1,0,2:T(8,128)(2,1)S(1)} copy(bf16[8,128,1408]{2,1,0:T(8,128)(2,1)} %param.7) | data formatting | bytes 5767168 | tf_op args[1]
  11.2 5.1 %abs_reduce_fusion.1 = f32[8,1408]{0,1:T(8,128)} fusion(f32[8,128,1408]{1,0,2:T(8,128)} %copy.69, bf16[8,128,1408]{1,0,2:T(8,128)(2,1)S(1)} %copy.68), kind=kLoop, calls=%fused_computation.5 | loop fusion | flops 5755904 | bytes 8695808 | tf_op jit(solution)/shard_map/reduce_max | solution.py:67
  16.3 1.3 copy.70
  17.6 6.5 %copy.72 = f32[8,128,1408]{1,0,2:T(8,128)} copy(f32[8,128,1408]{2,1,0:T(8,128)} %param.8) | data formatting | bytes 11534336 | tf_op args[2]
  24.1 4.9 %copy.71 = bf16[8,128,1408]{1,0,2:T(8,128)(2,1)} copy(bf16[8,128,1408]{2,1,0:T(8,128)(2,1)} %param.9) | data formatting | bytes 5767168 | tf_op args[3]
  29.0 0.0 copy-start
  29.0 5.6 %abs_reduce_fusion = f32[8,1408]{0,1:T(8,128)} fusion(f32[8,128,1408]{1,0,2:T(8,128)} %copy.72, bf16[8,128,1408]{1,0,2:T(8,128)(2,1)} %copy.71), kind=kLoop, calls=%fused_computation.3 | loop fusion | flops 5755904 | bytes 8695808 | tf_op jit(solution)/shard_map/reduce_max | solution.py:67
  34.6 1.3 copy.73
  35.9 1.8 %broadcast_in_dim.4 = f32[16,1,22528]{2,1,0:T(1,128)} broadcast(f32[22528]{0:T(1024)S(1)} %pad_maximum_fusion.1), dimensions={2} | broadcast | bytes 1531904 | tf_op jit(solution)/shard_map/broadcast_in_dim | solution.py:13
  37.8 8.2 %all-to-all-start = ((f32[16,1,22528]{2,1,0:T(1,128)}), f32[16,1,22528]{2,1,0:T(1,128)}, u32[]{:S(2)}, u32[]{:S(2)}) async-start(f32[16,1,22528]{2,1,0:T(1,128)} %broadcast_in_dim.4), calls=%async_computation | async-start | bytes 2883584 | tf_op jit(solution)/shard_map/all_to_all | solution.py:12
  46.0 0.0 copy-done
  46.0 0.0 copy-done.1
  46.1 19.1 %all-to-all-done = f32[16,1,22528]{2,1,0:T(1,128)} async-done(((f32[16,1,22528]{2,1,0:T(1,128)}), f32[16,1,22528]{2,1,0:T(1,128)}, u32[]{:S(2)}, u32[]{:S(2)}) %all-to-all-start) | async-done | bytes 1441824 | tf_op jit(solution)/shard_map/all_to_all | solution.py:12
  65.2 0.6 broadcast_in_dim.5
  65.8 6.5 %all-to-all-start.2 = ((bf16[16,128,8]{1,2,0:T(8,128)(2,1)}), bf16[16,128,8]{1,2,0:T(8,128)(2,1)S(1)}, u32[]{:S(2)}, u32[]{:S(2)}) async-start(bf16[16,128,8]{1,2,0:T(8,128)(2,1)} %broadcast_in_dim.5), calls=%async_computation.2 | async-start | bytes 65536 | tf_op jit(solution)/shard_map/all_to_all | solution.py:12
  72.3 2.3 %reduce_max.29 = f32[22528]{0:T(1024)S(1)} reduce(f32[16,1,22528]{2,1,0:T(1,128)} %all-to-all-done, f32[]{:T(128)} %constant.5.clone.1), dimensions={0,1}, to_apply=%region_2.0 | reduce | flops 337920 | bytes 1531908 | tf_op jit(solution)/shard_map/reduce_max | solution.py:19
  74.6 1.1 copy.75
  75.7 1.1 copy.76
  76.9 6.8 %divide_convert_fusion = (bf16[8,128,1408]{1,0,2:T(8,128)(2,1)S(1)}, bf16[8,128,1408]{1,0,2:T(8,128)(2,1)S(1)}) fusion(f32[8,128,1408]{1,0,2:T(8,128)} %copy.72, bf16[8,128,1408]{1,0,2:T(8,128)(2,1)} %copy.71, f32[8,1408]{0,1:T(8,128)} %copy.76, f32[8,1408]{0,1:T(8,128)} %copy.75, f32[8,128,1408]{1,0,2:T(8,128)} %copy.69, bf16[8,128,1408]{1,0,2:T(8,128)(2,1)S(1)} %copy.68), kind=kLoop, calls=%fused_computation.1 | loop fusion | flops 11534336 | bytes 23158784 | tf_op jit(solution)/shard_map/convert_element_type | solution.py:71
  83.7 3.2 %pad_maximum_fusion = bf16[16,128,1408]{1,0,2:T(8,128)(2,1)} fusion(bf16[8,128,1408]{1,0,2:T(8,128)(2,1)S(1)} %get-tuple-element.9, bf16[8,128,1408]{1,0,2:T(8,128)(2,1)S(1)} %get-tuple-element.10), kind=kLoop, calls=%fused_computation | loop fusion | flops 11534336 | bytes 11534336 | tf_op jit(solution)/shard_map/concatenate | solution.py:33
  86.9 0.0 all-to-all-done.2
  86.9 7.3 %all-to-all-start.1 = ((bf16[16,128,1408]{1,0,2:T(8,128)(2,1)}), bf16[16,128,1408]{1,0,2:T(8,128)(2,1)}, u32[]{:S(2)}, u32[]{:S(2)}) async-start(bf16[16,128,1408]{1,0,2:T(8,128)(2,1)} %pad_maximum_fusion), calls=%async_computation.1 | async-start | bytes 11534336 | tf_op jit(solution)/shard_map/all_to_all | solution.py:34
  94.2 64.7 %all_gather.6 = bf16[2,2048,8]{1,2,0:T(8,128)(2,1)S(1)} all-gather(bf16[1,2048,8]{1,2,0:T(8,128)(2,1)S(1)} %bitcast.27), channel_id=1, replica_groups=mesh['ep_0'=2,'ep_1'=4,'fsdp'=16] {'ep_0'}, dimensions={0}, use_global_device_ids=true | all-gather | bytes 98304 | tf_op jit(solution)/shard_map/all_gather | solution.py:52
  158.9 12.8 %all_gather.7 = bf16[8,2048,8]{1,2,0:T(8,128)(2,1)S(1)} all-gather(bf16[2,2048,8]{1,2,0:T(8,128)(2,1)S(1)} %all_gather.6), channel_id=1, replica_groups=mesh['ep_0'=2,'ep_1'=4,'fsdp'=16] {'ep_1'}, dimensions={0}, use_global_device_ids=true | all-gather | bytes 327680 | tf_op jit(solution)/shard_map/all_gather | solution.py:52
  171.7 0.7 copy.80
  172.4 0.7 constant_dynamic-slice_fusion
  173.1 0.0 all-to-all-done.1
  173.1 4.1 %copy.77 = bf16[16,128,1408]{1,2,0:T(8,128)(2,1)S(1)} copy(bf16[16,128,1408]{1,0,2:T(8,128)(2,1)} %all-to-all-done.1) | data formatting | bytes 11534336 | tf_op jit(solution)/shard_map/all_to_all | solution.py:34
  177.2 1.0 slice_bitcast_fusion
  178.2 2.4 %copy.88 = bf16[8,16,11,8,128]{4,3,1,2,0:T(8,128)(2,1)} copy(bf16[8,16,11,8,128]{4,3,2,1,0:T(8,128)(2,1)S(1)} %get-tuple-element.5) | data formatting | bytes 5767168 | tf_op jit(solution)/shard_map/split | solution.py:35
  180.6 2.4 %copy.89 = bf16[8,16,11,8,128]{4,3,1,2,0:T(8,128)(2,1)} copy(bf16[8,16,11,8,128]{4,3,2,1,0:T(8,128)(2,1)S(1)} %get-tuple-element.6) | data formatting | bytes 5767168 | tf_op jit(solution)/shard_map/split | solution.py:35
  (8 shorter events, 0.1 us)
Async XLA Ops:
  29.0 17.0 %copy-start = (f32[128,8]{0,1:T(8,128)S(1)}, f32[128,8]{0,1:T(8,128)}, u32[]{:S(2)}) copy-start(f32[128,8]{0,1:T(8,128)} %param.10) | copy-start | bytes 12292
  29.0 17.0 %copy-start.1 = (f32[128]{0:T(128)S(1)}, f32[128]{0:T(128)}, u32[]{:S(2)}) copy-start(f32[128]{0:T(128)} %param.11) | copy-start | bytes 1540
  37.8 27.4 %all-to-all-start = ((f32[16,1,22528]{2,1,0:T(1,128)}), f32[16,1,22528]{2,1,0:T(1,128)}, u32[]{:S(2)}, u32[]{:S(2)}) async-start(f32[16,1,22528]{2,1,0:T(1,128)} %broadcast_in_dim.4), calls=%async_computation | async-start | bytes 2883584 | tf_op jit(solution)/shard_map/all_to_all | solution.py:12
  65.8 21.1 %all-to-all-start.2 = ((bf16[16,128,8]{1,2,0:T(8,128)(2,1)}), bf16[16,128,8]{1,2,0:T(8,128)(2,1)S(1)}, u32[]{:S(2)}, u32[]{:S(2)}) async-start(bf16[16,128,8]{1,2,0:T(8,128)(2,1)} %broadcast_in_dim.5), calls=%async_computation.2 | async-start | bytes 65536 | tf_op jit(solution)/shard_map/all_to_all | solution.py:12
  86.9 86.1 %all-to-all-start.1 = ((bf16[16,128,1408]{1,0,2:T(8,128)(2,1)}), bf16[16,128,1408]{1,0,2:T(8,128)(2,1)}, u32[]{:S(2)}, u32[]{:S(2)}) async-start(bf16[16,128,1408]{1,0,2:T(8,128)(2,1)} %pad_maximum_fusion), calls=%async_computation.1 | async-start | bytes 11534336 | tf_op jit(solution)/shard_map/all_to_all | solution.py:34
where the time goes:
time: 184 us; the launch traced here: 183 us
  blocking collectives  77.5 us (42%)
  local copies, waits for them, and re-layouts  40.6 us (22%)
  other arithmetic  23 us (12%)
  starting transfers between devices  22 us (12%)
  waiting for transfers between devices  19.2 us (10%)
    all_gather x2, blocking collectives, stacked_from(): parts = lax.all_gather(parts, axes[k], axis=0, tiled=True)  77.5 us
    unnamed x9, local copies, waits for them, and re-layouts  22.9 us
    all_to_all x2, waiting for transfers between devices, sent_to_all(): lax.all_to_all(jnp.broadcast_to(array[None], (peers, *array.shape)), axis...  19.2 us
    all_to_all x2, starting transfers between devices, sent_to_all(): lax.all_to_all(jnp.broadcast_to(array[None], (peers, *array.shape)), axis...  14.7 us
    all_to_all x1, starting transfers between devices, side_by_side(): lax.all_to_all(both, axis, split_axis=split_dim, concat_axis=concat_dim,...  7.29 us
    convert_element_type x1, other arithmetic, per_device(): (latest_up / jnp.expand_dims(scale_up, 1)).astype(jnp.bfloat16)  6.79 us
    reduce_max x1, other arithmetic, per_device(): jnp.max(jnp.abs(latest_up), axis=1)  5.58 us
    reduce_max x1, other arithmetic, per_device(): jnp.max(jnp.abs(latest_gate), axis=1)  5.11 us
  transfers between devices with their start and end apart: 3, of which 1 were waited for; matrix products, arithmetic and copies ran while one was open for 9% of the time, Pallas kernels for 0%

commit v1 on v0

--- a/solution.py
+++ b/solution.py
@@ -5,6 +5,13 @@
 from jax.sharding import PartitionSpec as P
 
 EP = ("ep_0", "ep_1")
+
+
+def swapped_in(x, axis, d):
+    size = lax.axis_size(axis)
+    blocks = jnp.stack([x for _ in range(size)])
+    blocks = lax.all_to_all(blocks, axis, split_axis=0, concat_axis=0)
+    return jnp.concatenate(blocks, axis=d)
 
 
 def sent_to_all(array, axis):
@@ -49,7 +56,7 @@
 def stacked_from(array, axes, order):
     parts = array[None]
     for k in order:
-        parts = lax.all_gather(parts, axes[k], axis=0, tiled=True)
+        parts = swapped_in(parts, axes[k], 0)
     carried = [lax.axis_size(axes[k]) for k in reversed(order)]
     parts = parts.reshape(*carried, *array.shape)
     turned = sorted(range(len(order)), key=lambda place: order[len(order) - 1 - place])

time: 184 us -> 194 us (1.054)
  waiting for transfers between devices: 19.2 us -> 80.5 us
  blocking collectives: 77.5 us -> 26.1 us
    all_gather x2 -> x0, blocking collectives: 77.5 us -> none  [stacked_from(): parts = lax.all_gather(parts, axes[k], axis=0, tiled=True)]
    all_to_all x1, waiting for transfers between devices: 0.01 us -> 76.4 us  [side_by_side(): lax.all_to_all(both, axis, split_axis=split_dim, concat_axis=concat_dim,...]
    all_to_all x0 -> x1, blocking collectives: none -> 26.1 us  [sent_to_all(): lax.all_to_all(jnp.broadcast_to(array[None], (peers, *array.shape)), axis...]
    all_to_all x2 -> x1, waiting for transfers between devices: 19.2 us -> 0.01 us  [sent_to_all(): lax.all_to_all(jnp.broadcast_to(array[None], (peers, *array.shape)), axis...]
    all_to_all x0 -> x2, starting transfers between devices: none -> 7.59 us  [swapped_in(): blocks = lax.all_to_all(blocks, axis, split_axis=0, concat_axis=0)]
    all_to_all x2 -> x1, starting transfers between devices: 14.7 us -> 8.24 us  [sent_to_all(): lax.all_to_all(jnp.broadcast_to(array[None], (peers, *array.shape)), axis...]
    all_to_all x0 -> x2, waiting for transfers between devices: none -> 4.09 us  [swapped_in(): blocks = lax.all_to_all(blocks, axis, split_axis=0, concat_axis=0)]
    reduce_max x1, other arithmetic: 5.58 us -> 3.32 us  [per_device(): jnp.max(jnp.abs(latest_up), axis=1)]
  transfers between devices with their start and end apart: 3 -> 4, of which waited for: 1 -> 2; matrix products, arithmetic and copies ran while one was open for 9% -> 26% of each run, Pallas kernels for 0% -> 0%
where the time goes in v1:
time: 194 us; the launch traced here: 193 us
  waiting for transfers between devices  80.5 us (41%)
  local copies, waits for them, and re-layouts  39.9 us (21%)
  blocking collectives  26.1 us (13%)
  starting transfers between devices  23.2 us (12%)
  other arithmetic  22.7 us (12%)
    all_to_all x1, waiting for transfers between devices, side_by_side(): lax.all_to_all(both, axis, split_axis=split_dim, concat_axis=concat_dim,...  76.4 us
    all_to_all x1, blocking collectives, sent_to_all(): lax.all_to_all(jnp.broadcast_to(array[None], (peers, *array.shape)), axis...  26.1 us
    unnamed x15, local copies, waits for them, and re-layouts  22.4 us
    all_to_all x1, starting transfers between devices, sent_to_all(): lax.all_to_all(jnp.broadcast_to(array[None], (peers, *array.shape)), axis...  8.24 us
    all_to_all x2, starting transfers between devices, swapped_in(): blocks = lax.all_to_all(blocks, axis, split_axis=0, concat_axis=0)  7.59 us
    all_to_all x1, starting transfers between devices, side_by_side(): lax.all_to_all(both, axis, split_axis=split_dim, concat_axis=concat_dim,...  7.4 us
    convert_element_type x1, other arithmetic, per_device(): (latest_up / jnp.expand_dims(scale_up, 1)).astype(jnp.bfloat16)  6.8 us
    reduce_max x1, other arithmetic, per_device(): jnp.max(jnp.abs(latest_gate), axis=1)  5.75 us
  transfers between devices with their start and end apart: 4, of which 2 were waited for; matrix products, arithmetic and copies ran while one was open for 26% of the time, Pallas kernels for 0%

profile of v1, /device:TPU:8, one launch (start us, length us, event | category | flops | bytes accessed | tf_op | source)
XLA Modules:
  0.0 193.1 jit_solution(18240230069763889969)
XLA Ops:
  0.6 0.7 multiply_convert_fusion
  1.3 0.6 broadcast_in_dim.5
  1.9 8.2 %all-to-all-start.2 = ((bf16[16,128,8]{1,2,0:T(8,128)(2,1)}), bf16[16,128,8]{1,2,0:T(8,128)(2,1)S(1)}, u32[]{:S(2)}, u32[]{:S(2)}) async-start(bf16[16,128,8]{1,2,0:T(8,128)(2,1)} %broadcast_in_dim.5), calls=%async_computation.2 | async-start | bytes 65536 | tf_op jit(solution)/shard_map/all_to_all | solution.py:19
  10.2 6.6 %copy.76 = f32[8,128,1408]{1,0,2:T(8,128)} copy(f32[8,128,1408]{2,1,0:T(8,128)} %param.6) | data formatting | bytes 11534336 | tf_op args[0]
  16.8 3.4 %copy.75 = bf16[8,128,1408]{1,0,2:T(8,128)(2,1)} copy(bf16[8,128,1408]{2,1,0:T(8,128)(2,1)S(1)} %copy-done.2) | data formatting | bytes 5767168 | tf_op args[1]
  20.2 6.4 %copy.79 = f32[8,128,1408]{1,0,2:T(8,128)} copy(f32[8,128,1408]{2,1,0:T(8,128)} %param.8) | data formatting | bytes 11534336 | tf_op args[2]
  26.6 5.0 %copy.78 = bf16[8,128,1408]{1,0,2:T(8,128)(2,1)} copy(bf16[8,128,1408]{2,1,0:T(8,128)(2,1)} %param.9) | data formatting | bytes 5767168 | tf_op args[3]
  31.6 5.7 %abs_reduce_fusion.1 = f32[8,1408]{0,1:T(8,128)} fusion(f32[8,128,1408]{1,0,2:T(8,128)} %copy.76, bf16[8,128,1408]{1,0,2:T(8,128)(2,1)} %copy.75), kind=kLoop, calls=%fused_computation.5 | loop fusion | flops 5755904 | bytes 8695808 | tf_op jit(solution)/shard_map/reduce_max | solution.py:74
  37.3 3.3 %abs_reduce_fusion = f32[8,1408]{0,1:T(8,128)} fusion(f32[8,128,1408]{1,0,2:T(8,128)S(1)} %bitcast.23, bf16[8,128,1408]{1,0,2:T(8,128)(2,1)S(1)} %copy-done.1), kind=kLoop, calls=%fused_computation.3 | loop fusion | flops 5755904 | bytes 8695808 | tf_op jit(solution)/shard_map/reduce_max | solution.py:74
  40.7 1.5 copy.77
  42.1 1.3 copy.80
  43.5 0.6 pad_maximum_fusion.2
  44.2 3.3 %all-to-all-start.3 = ((bf16[2,1,2048,8]{2,3,1,0:T(8,128)(2,1)}), bf16[2,1,2048,8]{2,3,1,0:T(8,128)(2,1)S(1)}, u32[]{:S(2)}, u32[]{:S(2)}) async-start(bf16[2,1,2048,8]{2,3,1,0:T(8,128)(2,1)} %pad_maximum_fusion.2), calls=%async_computation.3 | async-start | bytes 131072 | tf_op jit(solution)/shard_map/all_to_all | solution.py:13
  47.5 4.1 %all-to-all-done.3 = bf16[2,1,2048,8]{2,3,1,0:T(8,128)(2,1)S(1)} async-done(((bf16[2,1,2048,8]{2,3,1,0:T(8,128)(2,1)}), bf16[2,1,2048,8]{2,3,1,0:T(8,128)(2,1)S(1)}, u32[]{:S(2)}, u32[]{:S(2)}) %all-to-all-start.3) | async-done | bytes 65568 | tf_op jit(solution)/shard_map/all_to_all | solution.py:13
  51.6 0.7 broadcast_in_dim.4
  52.3 26.1 %all_to_all.36 = f32[16,1,22528]{2,1,0:T(1,128)} all-to-all(f32[16,1,22528]{2,1,0:T(1,128)S(1)} %broadcast_in_dim.4), channel_id=1, replica_groups=mesh['ep_0'=2,'ep_1'=4,'fsdp'=16] {'fsdp'}, dimensions={0} | all-to-all | bytes 2883584 | tf_op jit(solution)/shard_map/all_to_all | solution.py:19
  78.4 0.7 stack.7
  79.1 4.3 %all-to-all-start.4 = ((bf16[4,2,2048,8]{2,3,1,0:T(8,128)(2,1)}), bf16[4,2,2048,8]{2,3,1,0:T(8,128)(2,1)S(1)}, u32[]{:S(2)}, u32[]{:S(2)}) async-start(bf16[4,2,2048,8]{2,3,1,0:T(8,128)(2,1)} %stack.7), calls=%async_computation.4 | async-start | bytes 524288 | tf_op jit(solution)/shard_map/all_to_all | solution.py:13
  83.4 2.3 %reduce_max.29 = f32[22528]{0:T(1024)S(1)} reduce(f32[16,1,22528]{2,1,0:T(1,128)} %all_to_all.36, f32[]{:T(128)} %constant.5.clone.1), dimensions={0,1}, to_apply=%region_2.0 | reduce | flops 337920 | bytes 1531908 | tf_op jit(solution)/shard_map/reduce_max | solution.py:26
  85.7 1.2 copy.82
  86.9 1.1 copy.83
  88.0 6.8 %divide_convert_fusion = (bf16[8,128,1408]{1,0,2:T(8,128)(2,1)S(1)}, bf16[8,128,1408]{1,0,2:T(8,128)(2,1)S(1)}) fusion(f32[8,128,1408]{1,0,2:T(8,128)} %copy.79, bf16[8,128,1408]{1,0,2:T(8,128)(2,1)} %copy.78, f32[8,1408]{0,1:T(8,128)} %copy.83, f32[8,1408]{0,1:T(8,128)} %copy.82, f32[8,128,1408]{1,0,2:T(8,128)} %copy.76, bf16[8,128,1408]{1,0,2:T(8,128)(2,1)S(1)} %copy-done), kind=kLoop, calls=%fused_computation.1 | loop fusion | flops 11534336 | bytes 23158784 | tf_op jit(solution)/shard_map/convert_element_type | solution.py:78
  94.8 3.2 %pad_maximum_fusion = bf16[16,128,1408]{1,0,2:T(8,128)(2,1)} fusion(bf16[8,128,1408]{1,0,2:T(8,128)(2,1)S(1)} %get-tuple-element.9, bf16[8,128,1408]{1,0,2:T(8,128)(2,1)S(1)} %get-tuple-element.10), kind=kLoop, calls=%fused_computation | loop fusion | flops 11534336 | bytes 11534336 | tf_op jit(solution)/shard_map/concatenate | solution.py:40
  98.0 0.0 all-to-all-done.4
  98.0 7.4 %all-to-all-start.1 = ((bf16[16,128,1408]{1,0,2:T(8,128)(2,1)}), bf16[16,128,1408]{1,0,2:T(8,128)(2,1)}, u32[]{:S(2)}, u32[]{:S(2)}) async-start(bf16[16,128,1408]{1,0,2:T(8,128)(2,1)} %pad_maximum_fusion), calls=%async_computation.1 | async-start | bytes 11534336 | tf_op jit(solution)/shard_map/all_to_all | solution.py:41
  105.4 0.7 copy.87
  106.1 0.7 constant_dynamic-slice_fusion
  106.8 76.4 %all-to-all-done.1 = bf16[16,128,1408]{1,0,2:T(8,128)(2,1)} async-done(((bf16[16,128,1408]{1,0,2:T(8,128)(2,1)}), bf16[16,128,1408]{1,0,2:T(8,128)(2,1)}, u32[]{:S(2)}, u32[]{:S(2)}) %all-to-all-start.1) | async-done | bytes 5767200 | tf_op jit(solution)/shard_map/all_to_all | solution.py:41
  183.2 4.1 %copy.84 = bf16[16,128,1408]{1,2,0:T(8,128)(2,1)S(1)} copy(bf16[16,128,1408]{1,0,2:T(8,128)(2,1)} %all-to-all-done.1) | data formatting | bytes 11534336 | tf_op jit(solution)/shard_map/all_to_all | solution.py:41
  187.4 1.0 slice_bitcast_fusion
  188.4 2.4 %copy.95 = bf16[8,16,11,8,128]{4,3,1,2,0:T(8,128)(2,1)} copy(bf16[8,16,11,8,128]{4,3,2,1,0:T(8,128)(2,1)S(1)} %get-tuple-element.5) | data formatting | bytes 5767168 | tf_op jit(solution)/shard_map/split | solution.py:42
  190.7 2.4 %copy.96 = bf16[8,16,11,8,128]{4,3,1,2,0:T(8,128)(2,1)} copy(bf16[8,16,11,8,128]{4,3,2,1,0:T(8,128)(2,1)S(1)} %get-tuple-element.6) | data formatting | bytes 5767168 | tf_op jit(solution)/shard_map/split | solution.py:42
  (18 shorter events, 0.1 us)
Async XLA Ops:
  1.9 41.6 %all-to-all-start.2 = ((bf16[16,128,8]{1,2,0:T(8,128)(2,1)}), bf16[16,128,8]{1,2,0:T(8,128)(2,1)S(1)}, u32[]{:S(2)}, u32[]{:S(2)}) async-start(bf16[16,128,8]{1,2,0:T(8,128)(2,1)} %broadcast_in_dim.5), calls=%async_computation.2 | async-start | bytes 65536 | tf_op jit(solution)/shard_map/all_to_all | solution.py:19
  10.2 6.6 %copy-start.2 = (bf16[8,128,1408]{2,1,0:T(8,128)(2,1)S(1)}, bf16[8,128,1408]{2,1,0:T(8,128)(2,1)}, u32[]{:S(2)}) copy-start(bf16[8,128,1408]{2,1,0:T(8,128)(2,1)} %param.7) | copy-start | bytes 8650756
  26.6 10.7 %slice-start = ((s8[5767168]{0:T(1024)(128)(4,1)}), s8[1572864]{0:T(1024)(128)(4,1)S(1)}, s32[]{:S(2)}) async-start(s8[5767168]{0:T(1024)(128)(4,1)} %bitcast.22), calls=%async_computation.5 | async-start | bytes 3145728
  31.6 5.8 %slice-start.1 = ((s8[5767168]{0:T(1024)(128)(4,1)}), s8[4194304]{0:T(1024)(128)(4,1)S(1)}, s32[]{:S(2)}) async-start(s8[5767168]{0:T(1024)(128)(4,1)} %bitcast.22), calls=%async_computation.6 | async-start | bytes 8388608
  31.6 5.8 %copy-start.1 = (bf16[8,128,1408]{1,0,2:T(8,128)(2,1)S(1)}, bf16[8,128,1408]{1,0,2:T(8,128)(2,1)}, u32[]{:S(2)}) copy-start(bf16[8,128,1408]{1,0,2:T(8,128)(2,1)} %copy.78) | copy-start | bytes 8650756
  40.7 47.3 %copy-start = (bf16[8,128,1408]{1,0,2:T(8,128)(2,1)S(1)}, bf16[8,128,1408]{1,0,2:T(8,128)(2,1)}, u32[]{:S(2)}) copy-start(bf16[8,128,1408]{1,0,2:T(8,128)(2,1)} %copy.75) | copy-start | bytes 8650756
  44.2 7.4 %all-to-all-start.3 = ((bf16[2,1,2048,8]{2,3,1,0:T(8,128)(2,1)}), bf16[2,1,2048,8]{2,3,1,0:T(8,128)(2,1)S(1)}, u32[]{:S(2)}, u32[]{:S(2)}) async-start(bf16[2,1,2048,8]{2,3,1,0:T(8,128)(2,1)} %pad_maximum_fusion.2), calls=%async_computation.3 | async-start | bytes 131072 | tf_op jit(solution)/shard_map/all_to_all | solution.py:13
  79.1 18.9 %all-to-all-start.4 = ((bf16[4,2,2048,8]{2,3,1,0:T(8,128)(2,1)}), bf16[4,2,2048,8]{2,3,1,0:T(8,128)(2,1)S(1)}, u32[]{:S(2)}, u32[]{:S(2)}) async-start(bf16[4,2,2048,8]{2,3,1,0:T(8,128)(2,1)} %stack.7), calls=%async_computation.4 | async-start | bytes 524288 | tf_op jit(solution)/shard_map/all_to_all | solution.py:13
  98.0 85.2 %all-to-all-start.1 = ((bf16[16,128,1408]{1,0,2:T(8,128)(2,1)}), bf16[16,128,1408]{1,0,2:T(8,128)(2,1)}, u32[]{:S(2)}, u32[]{:S(2)}) async-start(bf16[16,128,1408]{1,0,2:T(8,128)(2,1)} %pad_maximum_fusion), calls=%async_computation.1 | async-start | bytes 11534336 | tf_op jit(solution)/shard_map/all_to_all | solution.py:41
